TPU v7x, 8 devices: a whole 2x2x1 slice. The times are simulated.
8 devices in a mesh: data: 1 (over z), seq: 2 (over y), stage: 4 (over x, core).
Axes of the slice: x: 2, y: 2, z: 1, core: 2. Of those that a mesh axis runs over, the one named last changes fastest.
Arguments:
- x_init: float32 [2, 256, 48], P('data', 'seq')
- h_init: bfloat16 [3, 2, 256, 768], P(None, 'data', 'seq')
- w_in: bfloat16 [48, 768], replicated
- w_out: bfloat16 [768, 48], replicated
- w_qkv: bfloat16 [4, 768, 2304], P('stage')
- w_o: bfloat16 [4, 12, 64, 768], P('stage')
- w_up: bfloat16 [4, 768, 3072], P('stage')
- w_down: bfloat16 [4, 3072, 768], P('stage')
- ada_mod: float32 [4, 4, 6, 768], P(None, 'stage')
- alpha_coef: float32 [4], replicated
- beta_coef: float32 [4], replicated
Outputs:
- output 1: float32 [2, 256, 48], P('data', 'seq')
- output 2: bfloat16 [4, 2, 256, 768], P('stage', 'data', 'seq')
All inputs are finite; a program needn't handle non-finite values.
Results may differ from a plain program's by a relative error of at most 0.02.
Values are sent between devices in bfloat16 or wider.
A program may use at most 1 GiB of HBM per device.

v0:
```python
import functools

import jax
import jax.numpy as jnp
from jax import lax
from jax.experimental import pallas as pl
from jax.experimental.pallas import tpu as pltpu
from jax.sharding import PartitionSpec as P

LN_EPS = 1e-6
MESH = pl.DeviceIdType.MESH
BF16 = jnp.bfloat16
F32 = jnp.float32

STEPS = 4
STAGES = 4
DIM = 768
FF = 3072
HEADS = 12
HD = 64
ROWS = 128
LAT = 48
EXP2_SCALE = HD ** -0.5 * 1.4426950408889634
GELU_C0 = 0.7978845608028654
GELU_C1 = GELU_C0 * 0.044715


def layer_norm(hidden):
    mean_val = jnp.mean(hidden, axis=-1, keepdims=True)
    centered = hidden - mean_val
    variance = jnp.mean(centered * centered, axis=-1, keepdims=True)
    return centered * lax.rsqrt(variance + LN_EPS)


def gelu(val):
    half = 0.5 * val
    return half + half * jnp.tanh(val * (GELU_C0 + GELU_C1 * (val * val)))


def mm(lhs, rhs):
    return jnp.dot(lhs, rhs, preferred_element_type=F32)


def kernel(x_hbm, h_hbm, win_hbm, wout_hbm, wqkv_hbm, wo_hbm, wup_hbm, wdown_hbm, mod_hbm, alpha_ref, beta_ref,
           xo_ref, ho_hbm,
           wqkv, wo, wup, wdown, win, wout, mod, xraw, hin, outb, xbt, xbt_out, xs, xfin_out, xfin,
           hres, unorm, qkv, vt, attn, act,
           w_sem, small_sem, init_send, init_recv, st_send, st_recv, x_send, x_recv, xf_send, xf_recv, ho_sem, ho_send, ho_recv):
    y = lax.axis_index("seq")
    s = lax.axis_index("stage")
    z = lax.axis_index("data")
    oy = 1 - y
    is_first = s == 0
    is_last = s == STAGES - 1
    uses_x = jnp.logical_or(is_first, is_last)
    h_idx = jnp.maximum(s - 1, 0)

    def local(src, dst, sem):
        return pltpu.make_async_copy(src, dst, sem)

    def remote(src, dst, ssem, rsem, yy, ss):
        return pltpu.make_async_remote_copy(src_ref=src, dst_ref=dst, send_sem=ssem, recv_sem=rsem,
                                            device_id=(z, yy, ss), device_id_type=MESH)

    cp_h = local(h_hbm.at[h_idx, y], hin.at[0, 1], small_sem.at[0])
    cp_x = local(x_hbm.at[y], xraw.at[1], small_sem.at[1])
    cp_mod = local(mod_hbm, mod, small_sem.at[2])
    cp_win = local(win_hbm, win, small_sem.at[3])
    cp_wout = local(wout_hbm, wout, small_sem.at[4])
    cp_wqkv = local(wqkv_hbm, wqkv, w_sem.at[0])
    cp_wo = local(wo_hbm, wo, w_sem.at[1])
    cp_wup = local(wup_hbm, wup, w_sem.at[2])
    cp_wdown = local(wdown_hbm, wdown, w_sem.at[3])
    rc_h = remote(h_hbm.at[h_idx, oy], hin.at[0, 0], init_send.at[0], init_recv.at[0], oy, s)
    rc_x = remote(x_hbm.at[oy], xraw.at[0], init_send.at[1], init_recv.at[1], oy, s)

    @pl.when(jnp.logical_not(is_first))
    def _():
        cp_h.start()

    cp_x.start()
    cp_mod.start()
    cp_win.start()
    cp_wout.start()
    cp_wqkv.start()

    barrier = pltpu.get_barrier_semaphore()
    for dy in range(2):
        for ds in range(STAGES):
            if dy == 0 and ds == 0:
                continue
            pl.semaphore_signal(barrier, inc=1, device_id=(z, (y + dy) % 2, (s + ds) % STAGES), device_id_type=MESH)
    pl.semaphore_wait(barrier, 2 * STAGES - 1)

    @pl.when(jnp.logical_not(is_first))
    def _():
        rc_h.start()

    @pl.when(uses_x)
    def _():
        rc_x.start()

    cp_wo.start()
    cp_wup.start()
    cp_wdown.start()
    cp_x.wait()
    cp_mod.wait()
    cp_win.wait()
    cp_wout.wait()

    @pl.when(jnp.logical_not(is_first))
    def _():
        cp_h.wait()
        rc_h.wait_recv()

    @pl.when(uses_x)
    def _():
        rc_x.wait_recv()
        for c in range(2):
            xs[c] = xraw[c]
            xbt[0, c] = xraw[c].astype(BF16)

    cp_wqkv.wait()

    def stage_copy(k, c):
        return remote(outb.at[k, c], hin.at[k + 1, c], st_send.at[k, c], st_recv.at[k, c], y, s + 1)

    def x_copy(k, c):
        return remote(xbt_out.at[k, c], xbt.at[k + 1, c], x_send.at[k, c], x_recv.at[k, c], y, 0)

    def step(k, _):
        kprev = jnp.maximum(k - 1, 0)
        for c in range(2):
            @pl.when(jnp.logical_and(k > 0, jnp.logical_not(is_first)))
            def _():
                stage_copy(kprev, c).wait_recv()

            @pl.when(is_first)
            def _():
                @pl.when(k > 0)
                def _():
                    x_copy(kprev, c).wait_recv()
                xb = xbt[k, c].astype(F32).T.astype(BF16)
                hin[k, c] = mm(xb, win[...]).astype(BF16)

            h0 = hin[k, c].astype(F32)
            unorm[c] = (layer_norm(h0) * (1.0 + mod[k, 1]) + mod[k, 0]).astype(BF16)
            for n in range(0, 3 * DIM, 768):
                qkv[pl.ds(c * ROWS, ROWS), n:n + 768] = mm(unorm[c], wqkv[:, n:n + 768]).astype(BF16)

        for p in range(HEADS // 2):
            v2 = qkv[:, 2 * DIM + p * 128:2 * DIM + (p + 1) * 128]
            vt[pl.ds(p * 128, 128), :] = v2.T

        @pl.when(k == 0)
        def _():
            cp_wo.wait()
            cp_wup.wait()
            cp_wdown.wait()

        lane = lax.broadcasted_iota(jnp.int32, (ROWS, 128), 1)
        for c in range(2):
            rows = pl.ds(c * ROWS, ROWS)
            for p in range(HEADS // 2):
                q2 = qkv[rows, p * 128:(p + 1) * 128]
                k2 = qkv[:, DIM + p * 128:DIM + (p + 1) * 128]
                zero = jnp.zeros_like(q2)
                qq = jnp.concatenate([jnp.where(lane < HD, q2, zero), jnp.where(lane < HD, zero, q2)], axis=0)
                st = lax.dot_general(k2, qq, (((1,), (1,)), ((), ())), preferred_element_type=F32)
                mx = jnp.max(st, axis=0, keepdims=True)
                ex = jnp.exp2((st - mx) * EXP2_SCALE)
                inv = 1.0 / jnp.sum(ex, axis=0, keepdims=True)
                pt = (ex * inv).astype(BF16)
                ot = mm(vt[pl.ds(p * 128, 128), :], pt)
                o2 = jnp.concatenate([ot[:HD, :ROWS], ot[HD:, ROWS:]], axis=0)
                attn[:, p * 128:(p + 1) * 128] = o2.T.astype(BF16)
            h1 = hin[k, c].astype(F32) + mod[k, 2] * mm(attn[...], wo[...])
            hres[...] = h1
            u2 = (layer_norm(h1) * (1.0 + mod[k, 4]) + mod[k, 3]).astype(BF16)
            unorm[c] = u2
            for n in range(0, FF, 512):
                act[:, n:n + 512] = gelu(mm(unorm[c], wup[:, n:n + 512])).astype(BF16)
            h2 = hres[...] + mod[k, 5] * mm(act[...], wdown[...])
            out = h2.astype(BF16)
            outb[k, c] = out

            @pl.when(jnp.logical_and(k < STEPS - 1, jnp.logical_not(is_last)))
            def _():
                stage_copy(k, c).start()

            if c == 0:
                @pl.when(k == STEPS - 1)
                def _():
                    remote(outb.at[k, c], ho_hbm.at[y], ho_send, ho_recv, oy, s).start()
            else:
                @pl.when(k == STEPS - 1)
                def _():
                    local(outb.at[k, c], ho_hbm.at[y], ho_sem).start()

            @pl.when(is_last)
            def _():
                eps = lax.dot_general(wout[...], outb[k, c], (((1,), (1,)), ((), ())), preferred_element_type=F32)
                xn = alpha_ref[k] * xs[c] + beta_ref[k] * eps
                xs[c] = xn

                @pl.when(k < STEPS - 1)
                def _():
                    xbt_out[k, c] = xn.astype(BF16)
                    x_copy(k, c).start()

                @pl.when(k == STEPS - 1)
                def _():
                    xfin_out[c] = xn
                    if c == 0:
                        for t in range(STAGES):
                            remote(xfin_out.at[c], xfin.at[y], xf_send.at[t], xf_recv.at[y], oy, t).start()
                    else:
                        for t in range(STAGES - 1):
                            remote(xfin_out.at[c], xfin.at[y], xf_send.at[STAGES + t], xf_recv.at[y], y, t).start()
                        xfin[y] = xn
        return 0

    lax.fori_loop(0, STEPS, step, 0)

    remote(xfin_out.at[0], xfin.at[oy], xf_send.at[0], xf_recv.at[oy], oy, s).wait_recv()

    @pl.when(jnp.logical_not(is_last))
    def _():
        remote(xfin_out.at[0], xfin.at[y], xf_send.at[0], xf_recv.at[y], y, s).wait_recv()

    for b in range(2):
        xo_ref[b] = xfin[b]

    @pl.when(is_last)
    def _():
        for t in range(STAGES):
            remote(xfin_out.at[0], xfin.at[y], xf_send.at[t], xf_recv.at[y], oy, t).wait_send()
        for t in range(STAGES - 1):
            remote(xfin_out.at[1], xfin.at[y], xf_send.at[STAGES + t], xf_recv.at[y], y, t).wait_send()
        for k in range(STEPS - 1):
            for c in range(2):
                x_copy(k, c).wait_send()

    @pl.when(jnp.logical_not(is_last))
    def _():
        for k in range(STEPS - 1):
            for c in range(2):
                stage_copy(k, c).wait_send()

    @pl.when(jnp.logical_not(is_first))
    def _():
        rc_h.wait_send()

    @pl.when(uses_x)
    def _():
        rc_x.wait_send()

    local(outb.at[STEPS - 1, 1], ho_hbm.at[y], ho_sem).wait()
    last = remote(outb.at[STEPS - 1, 0], ho_hbm.at[oy], ho_send, ho_recv, oy, s)
    last.wait_send()
    last.wait_recv()


def solution(mesh):
    hbm = pl.BlockSpec(memory_space=pltpu.HBM)
    smem = pl.BlockSpec(memory_space=pltpu.SMEM)
    vmem = pl.BlockSpec(memory_space=pltpu.VMEM)
    dma = pltpu.SemaphoreType.DMA
    scratch = [
        pltpu.VMEM((DIM, 3 * DIM), BF16),
        pltpu.VMEM((DIM, DIM), BF16),
        pltpu.VMEM((DIM, FF), BF16),
        pltpu.VMEM((FF, DIM), BF16),
        pltpu.VMEM((LAT, DIM), BF16),
        pltpu.VMEM((LAT, DIM), BF16),
        pltpu.VMEM((STEPS, 6, 1, DIM), F32),
        pltpu.VMEM((2, LAT, ROWS), F32),
        pltpu.VMEM((STEPS, 2, ROWS, DIM), BF16),
        pltpu.VMEM((STEPS, 2, ROWS, DIM), BF16),
        pltpu.VMEM((STEPS, 2, LAT, ROWS), BF16),
        pltpu.VMEM((STEPS, 2, LAT, ROWS), BF16),
        pltpu.VMEM((2, LAT, ROWS), F32),
        pltpu.VMEM((2, LAT, ROWS), F32),
        pltpu.VMEM((2, LAT, ROWS), F32),
        pltpu.VMEM((ROWS, DIM), F32),
        pltpu.VMEM((2, ROWS, DIM), BF16),
        pltpu.VMEM((2 * ROWS, 3 * DIM), BF16),
        pltpu.VMEM((DIM, 2 * ROWS), BF16),
        pltpu.VMEM((ROWS, DIM), BF16),
        pltpu.VMEM((ROWS, FF), BF16),
        dma((4,)), dma((5,)), dma((2,)), dma((2,)),
        dma((STEPS - 1, 2)), dma((STEPS - 1, 2)), dma((STEPS - 1, 2)), dma((STEPS - 1, 2)),
        dma((2 * STAGES - 1,)), dma((2,)), dma, dma, dma,
    ]

    def device_fn(x_init, h_init, w_in, w_out, w_qkv, w_o, w_up, w_down, ada_mod, alpha_coef, beta_coef):
        call = pl.pallas_call(
            kernel,
            name="dit_steps",
            out_shape=(jax.ShapeDtypeStruct((2, LAT, ROWS), F32), jax.ShapeDtypeStruct((2, ROWS, DIM), BF16)),
            in_specs=[hbm] * 9 + [smem] * 2,
            out_specs=(vmem, hbm),
            scratch_shapes=scratch,
            compiler_params=pltpu.CompilerParams(collective_id=0, has_side_effects=True, vmem_limit_bytes=60 * 1024 * 1024),
        )
        x_final, h_final = call(x_init.swapaxes(1, 2), h_init, w_in, w_out.T, w_qkv.reshape(DIM, 3 * DIM), w_o.reshape(DIM, DIM),
                                w_up.reshape(DIM, FF), w_down.reshape(FF, DIM), ada_mod.swapaxes(1, 2), alpha_coef, beta_coef)
        return x_final.swapaxes(1, 2), h_final[None]

    weight_spec = P("stage", None, None)
    return jax.shard_map(
        device_fn,
        mesh=mesh,
        in_specs=(P("data", "seq", None), P(None, "data", "seq", None), P(), P(), weight_spec, P("stage", None, None, None), weight_spec, weight_spec, P(None, "stage", None, None), P(), P()),
        out_specs=(P("data", "seq", None), P("stage", "data", "seq", None)),
        check_vma=False,
    )
```

profile of v0, /device:TPU:0, one launch (start us, length us, event | category | flops | bytes accessed | tf_op | source)
XLA Modules:
  0.0 60.5 jit_solution(867262185849803566)
XLA Ops:
  0.6 56.7 %dit_steps.1 = (f32[2,48,128]{2,1,0:T(8,128)}, bf16[2,128,768]{2,1,0:T(8,128)(2,1)}) custom-call(f32[2,48,128]{2,1,0:T(8,128)} %bitcast.16, bf16[3,2,128,768]{3,2,1,0:T(8,128)(2,1)} %h_hbm.1, bf16[48,768]{1,0:T(8,128)(2,1)} %win_hbm.1, bf16[48,768]{1,0:T(8,128)(2,1)} %bitcast.14, bf16[768,2304]{1,0:T(8,128)(2,1)} %bitcast.11, bf16[768,768]{1,0:T(8,128)(2,1)} %bitcast.12, ...), custom_call_target="tpu_custom_call" | custom-call | tf_op jit(solution)/shard_map/dit_steps/pallas_call | solution.py:306
  57.3 1.4 %copy.15 = f32[2,128,48]{1,2,0:T(8,128)} copy(f32[2,128,48]{1,2,0:T(8,128)} %bitcast.17) | data formatting | bytes 98304
  58.8 1.8 %copy.16 = bf16[1,2,128,768]{3,2,1,0:T(8,128)(2,1)} copy(bf16[1,2,128,768]{3,2,1,0:T(8,128)(2,1)} %bitcast.13) | data formatting | bytes 786432
where the time goes:
time: 60.7 us; the launch traced here: 60.5 us
  Pallas kernels  56.7 us (93%)
  local copies, waits for them, and re-layouts  3.19 us (5%)
  between operations  0.64 us (1%)
    pallas_call x1, Pallas kernels, device_fn(): call(x_init.swapaxes(1, 2), h_init, w_in, w_out.T, w_qkv.reshape(DIM, 3 *...  56.7 us
    unnamed x2, local copies, waits for them, and re-layouts  3.19 us

commit v1 on v0

v1 whole, which is shorter than its diff:
```python
import functools

import jax
import jax.numpy as jnp
from jax import lax
from jax.experimental import pallas as pl
from jax.experimental.pallas import tpu as pltpu
from jax.sharding import PartitionSpec as P

LN_EPS = 1e-6
MESH = pl.DeviceIdType.MESH
BF16 = jnp.bfloat16
F32 = jnp.float32

STEPS = 4
STAGES = 4
DIM = 768
FF = 3072
HEADS = 12
HD = 64
ROWS = 128
LAT = 48
EXP2_SCALE = HD ** -0.5 * 1.4426950408889634
GELU_C0 = 0.7978845608028654
GELU_C1 = GELU_C0 * 0.044715


def layer_norm(hidden):
    mean_val = jnp.mean(hidden, axis=-1, keepdims=True)
    centered = hidden - mean_val
    variance = jnp.mean(centered * centered, axis=-1, keepdims=True)
    return centered * lax.rsqrt(variance + LN_EPS)


def gelu(val):
    half = 0.5 * val
    return half + half * jnp.tanh(val * (GELU_C0 + GELU_C1 * (val * val)))


def mm(lhs, rhs):
    return jnp.dot(lhs, rhs, preferred_element_type=F32)


def interleave(*streams):
    order = []
    for idx, pieces in enumerate(streams):
        for pos in range(len(pieces)):
            order.append(((pos + 0.5) / len(pieces), idx, pos))
    for _, idx, pos in sorted(order):
        streams[idx][pos]()


def kernel(x_hbm, h_hbm, win_hbm, wout_hbm, wqkv_hbm, wo_hbm, wup_hbm, wdown_hbm, mod_hbm, alpha_ref, beta_ref,
           xo_ref, ho_hbm,
           wqkv, wo, wup, wdown, win, wout, mod, xraw, hin, outb, xbt, xbt_out, xs, xfin_out, xfin,
           hres, unorm, qs, ks, vt, attn, act, s_a, s_b, p_a, p_b,
           w_sem, small_sem, init_send, init_recv, st_send, st_recv, x_send, x_recv, xf_send, xf_recv, ho_sem, ho_send, ho_recv, go_sem):
    y = lax.axis_index("seq")
    s = lax.axis_index("stage")
    z = lax.axis_index("data")
    oy = 1 - y
    is_first = s == 0
    is_last = s == STAGES - 1
    is_waiter = s == STAGES - 2
    uses_x = jnp.logical_or(is_first, is_last)
    h_idx = jnp.maximum(s - 1, 0)

    def local(src, dst, sem):
        return pltpu.make_async_copy(src, dst, sem)

    def remote(src, dst, ssem, rsem, yy, ss):
        return pltpu.make_async_remote_copy(src_ref=src, dst_ref=dst, send_sem=ssem, recv_sem=rsem,
                                            device_id=(z, yy, ss), device_id_type=MESH)

    cp_h = local(h_hbm.at[h_idx, y], hin.at[0, 1], small_sem.at[0])
    cp_x = local(x_hbm.at[y], xraw.at[1], small_sem.at[1])
    cp_mod = local(mod_hbm, mod, small_sem.at[2])
    cp_win = local(win_hbm, win, small_sem.at[3])
    cp_wout = local(wout_hbm, wout, small_sem.at[4])
    cp_wqkv = [local(wqkv_hbm.at[:, pl.ds(j * DIM, DIM)], wqkv.at[j], w_sem.at[j]) for j in range(3)]
    cp_rest = [local(wo_hbm, wo, w_sem.at[3])]
    cp_rest += [local(wup_hbm.at[:, pl.ds(j * DIM, DIM)], wup.at[j], w_sem.at[4 + j]) for j in range(4)]
    cp_rest += [local(wdown_hbm, wdown, w_sem.at[8])]
    rc_h = remote(h_hbm.at[h_idx, oy], hin.at[0, 0], init_send.at[0], init_recv.at[0], oy, s)
    rc_x = remote(x_hbm.at[oy], xraw.at[0], init_send.at[1], init_recv.at[1], oy, s)

    @pl.when(jnp.logical_not(is_first))
    def _():
        cp_h.start()

    cp_x.start()
    cp_mod.start()
    cp_win.start()
    cp_wout.start()
    for j in (1, 2, 0):
        cp_wqkv[j].start()

    barrier = pltpu.get_barrier_semaphore()
    for dy in range(2):
        for ds in range(STAGES):
            if dy == 0 and ds == 0:
                continue
            pl.semaphore_signal(barrier, inc=1, device_id=(z, (y + dy) % 2, (s + ds) % STAGES), device_id_type=MESH)
    pl.semaphore_wait(barrier, 2 * STAGES - 1)

    @pl.when(uses_x)
    def _():
        rc_x.start()

    @pl.when(jnp.logical_not(jnp.logical_or(is_first, is_waiter)))
    def _():
        rc_h.start()

    for cp in cp_rest:
        cp.start()

    @pl.when(is_last)
    def _():
        rc_h.wait_send()
        pl.semaphore_signal(go_sem, inc=1, device_id=(z, y, s - 1), device_id_type=MESH)

    @pl.when(is_waiter)
    def _():
        pl.semaphore_wait(go_sem, 1)
        rc_h.start()

    cp_x.wait()
    cp_mod.wait()
    cp_win.wait()
    cp_wout.wait()

    @pl.when(jnp.logical_not(is_first))
    def _():
        cp_h.wait()

    @pl.when(uses_x)
    def _():
        xs[1] = xraw[1]
        xbt[0, 1] = xraw[1].astype(BF16)

    for cp in cp_wqkv:
        cp.wait()

    def stage_copy(k, c):
        return remote(outb.at[k, c], hin.at[k + 1, c], st_send.at[k, c], st_recv.at[k, c], y, s + 1)

    def x_copy(k, c):
        return remote(xbt_out.at[k, c], xbt.at[k + 1, c], x_send.at[k, c], x_recv.at[k, c], y, 0)

    lane = lax.broadcasted_iota(jnp.int32, (ROWS, 128), 1)
    PAIRS = HEADS // 2
    LNB = 32

    def embed(k, c):
        @pl.when(is_first)
        def _():
            xb = xbt[k, c].astype(F32).T.astype(BF16)
            hin[k, c] = mm(xb, win[...]).astype(BF16)

    def ln1_pieces(k, c):
        def piece(r):
            def run():
                rows = pl.ds(r, LNB)
                h0 = hin[k, c, rows].astype(F32)
                unorm[c, rows] = (layer_norm(h0) * (1.0 + mod[k, 1]) + mod[k, 0]).astype(BF16)
            return run
        return [piece(r) for r in range(0, ROWS, LNB)]

    def q_pieces(c):
        def piece(n):
            def run():
                qs[c, :, n:n + 256] = mm(unorm[c], wqkv[0, :, n:n + 256]).astype(BF16)
            return run
        return [piece(n) for n in range(0, DIM, 256)]

    def k_pieces(c):
        def piece(n):
            def run():
                ks[c, :, n:n + 256] = mm(unorm[c], wqkv[1, :, n:n + 256]).astype(BF16)
            return run
        return [piece(n) for n in range(0, DIM, 256)]

    def v_pieces(c):
        def piece(n):
            def run():
                val = mm(unorm[c], wqkv[2, :, n:n + 256])
                vt[c, n:n + 256, :] = val.T.astype(BF16)
            return run
        return [piece(n) for n in range(0, DIM, 256)]

    def attn_pieces(c):
        s_scr, p_scr = (s_a, s_b), (p_a, p_b)

        def scores(p):
            cols = slice(p * 128, (p + 1) * 128)
            q2 = qs[c, :, cols]
            zero = jnp.zeros_like(q2)
            qq = jnp.concatenate([jnp.where(lane < HD, q2, zero), jnp.where(lane < HD, zero, q2)], axis=0)
            k2 = jnp.concatenate([ks[0, :, cols], ks[1, :, cols]], axis=0)
            s_scr[p % 2][...] = lax.dot_general(k2, qq, (((1,), (1,)), ((), ())), preferred_element_type=F32)

        def softmax(p, half):
            cols = slice(half * ROWS, (half + 1) * ROWS)
            st = s_scr[p % 2][:, cols]
            mx = jnp.max(st, axis=0, keepdims=True)
            ex = jnp.exp2((st - mx) * EXP2_SCALE)
            inv = 1.0 / jnp.sum(ex, axis=0, keepdims=True)
            p_scr[p % 2][:, cols] = (ex * inv).astype(BF16)

        def values(p):
            cols = slice(p * 128, (p + 1) * 128)
            v2 = jnp.concatenate([vt[0, cols, :], vt[1, cols, :]], axis=1)
            ot = mm(v2, p_scr[p % 2][...])
            o2 = jnp.concatenate([ot[:HD, :ROWS], ot[HD:, ROWS:]], axis=0)
            attn[c, :, cols] = o2.T.astype(BF16)

        pieces = [functools.partial(scores, 0)]
        for p in range(PAIRS):
            if p + 1 < PAIRS:
                pieces.append(functools.partial(scores, p + 1))
            pieces.append(functools.partial(softmax, p, 0))
            pieces.append(functools.partial(softmax, p, 1))
            pieces.append(functools.partial(values, p))
        return pieces

    def wo_pieces(c):
        def piece(n):
            def run():
                hres[c, :, n:n + 256] = mm(attn[c], wo[:, n:n + 256])
            return run
        return [piece(n) for n in range(0, DIM, 256)]

    def ln2_pieces(k, c):
        def piece(r):
            def run():
                rows = pl.ds(r, LNB)
                h1 = hin[k, c, rows].astype(F32) + mod[k, 2] * hres[c, rows]
                hres[c, rows] = h1
                unorm[c, rows] = (layer_norm(h1) * (1.0 + mod[k, 4]) + mod[k, 3]).astype(BF16)
            return run
        return [piece(r) for r in range(0, ROWS, LNB)]

    def up_pieces(c):
        def piece(n):
            def run():
                j, m = divmod(n, DIM)
                act[c, :, n:n + 256] = gelu(mm(unorm[c], wup[j, :, m:m + 256])).astype(BF16)
            return run
        return [piece(n) for n in range(0, FF, 256)]

    def down_pieces(k, c):
        def store(n, res):
            out = hres[c, :, n:n + 256] + mod[k, 5][:, n:n + 256] * res
            outb[k, c, :, n:n + 256] = out.astype(BF16)

        def full(n):
            def run():
                store(n, mm(act[c], wdown[:, n:n + 256]))
            return run

        def halves(n):
            def run():
                lo = mm(act[c, :, :FF // 2], wdown[:FF // 2, n:n + 256])
                hi = mm(act[c, :, FF // 2:], wdown[FF // 2:, n:n + 256])
                store(n, lo + hi)
            return run
        return [full(0), full(256), halves(512)]

    def finish(k, c):
        @pl.when(jnp.logical_and(k < STEPS - 1, jnp.logical_not(is_last)))
        def _():
            stage_copy(k, c).start()

        if c == 0:
            @pl.when(k == STEPS - 1)
            def _():
                remote(outb.at[k, c], ho_hbm.at[y], ho_send, ho_recv, oy, s).start()
        else:
            @pl.when(k == STEPS - 1)
            def _():
                local(outb.at[k, c], ho_hbm.at[y], ho_sem).start()

        @pl.when(is_last)
        def _():
            eps = lax.dot_general(wout[...], outb[k, c], (((1,), (1,)), ((), ())), preferred_element_type=F32)
            xn = alpha_ref[k] * xs[c] + beta_ref[k] * eps
            xs[c] = xn

            @pl.when(k < STEPS - 1)
            def _():
                xbt_out[k, c] = xn.astype(BF16)
                x_copy(k, c).start()

            @pl.when(k == STEPS - 1)
            def _():
                xfin_out[c] = xn
                if c == 0:
                    for t in range(STAGES):
                        remote(xfin_out.at[c], xfin.at[y], xf_send.at[t], xf_recv.at[y], oy, t).start()
                else:
                    for t in range(STAGES - 1):
                        remote(xfin_out.at[c], xfin.at[y], xf_send.at[STAGES + t], xf_recv.at[y], y, t).start()
                    xfin[y] = xn

    def step(k, _):
        kprev = jnp.maximum(k - 1, 0)
        ca = jnp.where(k == 0, 1, 0)
        cb = 1 - ca

        @pl.when(jnp.logical_and(k > 0, jnp.logical_not(is_first)))
        def _():
            stage_copy(kprev, ca).wait_recv()

        @pl.when(jnp.logical_and(k > 0, is_first))
        def _():
            x_copy(kprev, ca).wait_recv()

        embed(k, ca)
        interleave(ln1_pieces(k, ca))
        interleave(k_pieces(ca) + v_pieces(ca))

        @pl.when(jnp.logical_and(k > 0, jnp.logical_not(is_first)))
        def _():
            stage_copy(kprev, cb).wait_recv()

        @pl.when(jnp.logical_and(k > 0, is_first))
        def _():
            x_copy(kprev, cb).wait_recv()

        @pl.when(k == 0)
        def _():
            @pl.when(jnp.logical_not(is_first))
            def _():
                rc_h.wait_recv()

            @pl.when(uses_x)
            def _():
                rc_x.wait_recv()
                xs[0] = xraw[0]
                xbt[0, 0] = xraw[0].astype(BF16)

            for cp in cp_rest:
                cp.wait()

        embed(k, cb)
        interleave(q_pieces(ca), ln1_pieces(k, cb))
        interleave(k_pieces(cb))
        interleave(q_pieces(cb))
        interleave(v_pieces(cb))
        interleave(attn_pieces(0))
        att1 = attn_pieces(1)
        interleave(wo_pieces(0) + ln2_pieces(k, 0), att1[:8])
        interleave(up_pieces(0))
        interleave(down_pieces(k, 0), att1[8:])
        finish(k, 0)
        interleave(wo_pieces(1))
        interleave(ln2_pieces(k, 1))
        interleave(up_pieces(1))
        interleave(down_pieces(k, 1))
        finish(k, 1)
        return 0

    lax.fori_loop(0, STEPS, step, 0)

    remote(xfin_out.at[0], xfin.at[oy], xf_send.at[0], xf_recv.at[oy], oy, s).wait_recv()

    @pl.when(jnp.logical_not(is_last))
    def _():
        remote(xfin_out.at[0], xfin.at[y], xf_send.at[0], xf_recv.at[y], y, s).wait_recv()

    for b in range(2):
        xo_ref[b] = xfin[b]

    @pl.when(is_last)
    def _():
        for t in range(STAGES):
            remote(xfin_out.at[0], xfin.at[y], xf_send.at[t], xf_recv.at[y], oy, t).wait_send()
        for t in range(STAGES - 1):
            remote(xfin_out.at[1], xfin.at[y], xf_send.at[STAGES + t], xf_recv.at[y], y, t).wait_send()
        for k in range(STEPS - 1):
            for c in range(2):
                x_copy(k, c).wait_send()

    @pl.when(jnp.logical_not(is_last))
    def _():
        for k in range(STEPS - 1):
            for c in range(2):
                stage_copy(k, c).wait_send()

    @pl.when(jnp.logical_not(jnp.logical_or(is_first, is_last)))
    def _():
        rc_h.wait_send()

    @pl.when(uses_x)
    def _():
        rc_x.wait_send()

    local(outb.at[STEPS - 1, 1], ho_hbm.at[y], ho_sem).wait()
    last = remote(outb.at[STEPS - 1, 0], ho_hbm.at[oy], ho_send, ho_recv, oy, s)
    last.wait_send()
    last.wait_recv()


def solution(mesh):
    hbm = pl.BlockSpec(memory_space=pltpu.HBM)
    smem = pl.BlockSpec(memory_space=pltpu.SMEM)
    vmem = pl.BlockSpec(memory_space=pltpu.VMEM)
    dma = pltpu.SemaphoreType.DMA
    scratch = [
        pltpu.VMEM((3, DIM, DIM), BF16),
        pltpu.VMEM((DIM, DIM), BF16),
        pltpu.VMEM((4, DIM, DIM), BF16),
        pltpu.VMEM((FF, DIM), BF16),
        pltpu.VMEM((LAT, DIM), BF16),
        pltpu.VMEM((LAT, DIM), BF16),
        pltpu.VMEM((STEPS, 6, 1, DIM), F32),
        pltpu.VMEM((2, LAT, ROWS), F32),
        pltpu.VMEM((STEPS, 2, ROWS, DIM), BF16),
        pltpu.VMEM((STEPS, 2, ROWS, DIM), BF16),
        pltpu.VMEM((STEPS, 2, LAT, ROWS), BF16),
        pltpu.VMEM((STEPS, 2, LAT, ROWS), BF16),
        pltpu.VMEM((2, LAT, ROWS), F32),
        pltpu.VMEM((2, LAT, ROWS), F32),
        pltpu.VMEM((2, LAT, ROWS), F32),
        pltpu.VMEM((2, ROWS, DIM), F32),
        pltpu.VMEM((2, ROWS, DIM), BF16),
        pltpu.VMEM((2, ROWS, DIM), BF16),
        pltpu.VMEM((2, ROWS, DIM), BF16),
        pltpu.VMEM((2, DIM, ROWS), BF16),
        pltpu.VMEM((2, ROWS, DIM), BF16),
        pltpu.VMEM((2, ROWS, FF), BF16),
        pltpu.VMEM((2 * ROWS, 2 * ROWS), F32),
        pltpu.VMEM((2 * ROWS, 2 * ROWS), F32),
        pltpu.VMEM((2 * ROWS, 2 * ROWS), BF16),
        pltpu.VMEM((2 * ROWS, 2 * ROWS), BF16),
        dma((9,)), dma((5,)), dma((2,)), dma((2,)),
        dma((STEPS - 1, 2)), dma((STEPS - 1, 2)), dma((STEPS - 1, 2)), dma((STEPS - 1, 2)),
        dma((2 * STAGES - 1,)), dma((2,)), dma, dma, dma, pltpu.SemaphoreType.REGULAR,
    ]

    def device_fn(x_init, h_init, w_in, w_out, w_qkv, w_o, w_up, w_down, ada_mod, alpha_coef, beta_coef):
        call = pl.pallas_call(
            kernel,
            name="dit_steps",
            out_shape=(jax.ShapeDtypeStruct((2, LAT, ROWS), F32), jax.ShapeDtypeStruct((2, ROWS, DIM), BF16)),
            in_specs=[hbm] * 9 + [smem] * 2,
            out_specs=(vmem, hbm),
            scratch_shapes=scratch,
            compiler_params=pltpu.CompilerParams(collective_id=0, has_side_effects=True, vmem_limit_bytes=60 * 1024 * 1024),
        )
        x_final, h_final = call(x_init.swapaxes(1, 2), h_init, w_in, w_out.T, w_qkv.reshape(DIM, 3 * DIM), w_o.reshape(DIM, DIM),
                                w_up.reshape(DIM, FF), w_down.reshape(FF, DIM), ada_mod.swapaxes(1, 2), alpha_coef, beta_coef)
        return x_final.swapaxes(1, 2), h_final[None]

    weight_spec = P("stage", None, None)
    return jax.shard_map(
        device_fn,
        mesh=mesh,
        in_specs=(P("data", "seq", None), P(None, "data", "seq", None), P(), P(), weight_spec, P("stage", None, None, None), weight_spec, weight_spec, P(None, "stage", None, None), P(), P()),
        out_specs=(P("data", "seq", None), P("stage", "data", "seq", None)),
        check_vma=False,
    )
```

time: 60.7 us -> 53.4 us (0.88)
  Pallas kernels: 56.7 us -> 49.4 us
    pallas_call x1, Pallas kernels: 56.7 us -> 49.4 us  [device_fn(): call(x_init.swapaxes(1, 2), h_init, w_in, w_out.T, w_qkv.reshape(DIM, 3 *...]
where the time goes in v1:
time: 53.4 us; the launch traced here: 53.2 us
  Pallas kernels  49.4 us (93%)
  local copies, waits for them, and re-layouts  3.19 us (6%)
  between operations  0.64 us (1%)
    pallas_call x1, Pallas kernels, device_fn(): call(x_init.swapaxes(1, 2), h_init, w_in, w_out.T, w_qkv.reshape(DIM, 3 *...  49.4 us
    unnamed x2, local copies, waits for them, and re-layouts  3.19 us

profile of v1, /device:TPU:0, one launch (start us, length us, event | category | flops | bytes accessed | tf_op | source)
XLA Modules:
  0.0 53.2 jit_solution(7616834213785414821)
XLA Ops:
  0.6 49.4 %dit_steps.1 = (f32[2,48,128]{2,1,0:T(8,128)}, bf16[2,128,768]{2,1,0:T(8,128)(2,1)}) custom-call(f32[2,48,128]{2,1,0:T(8,128)} %bitcast.16, bf16[3,2,128,768]{3,2,1,0:T(8,128)(2,1)} %h_hbm.1, bf16[48,768]{1,0:T(8,128)(2,1)} %win_hbm.1, bf16[48,768]{1,0:T(8,128)(2,1)} %bitcast.14, bf16[768,2304]{1,0:T(8,128)(2,1)} %bitcast.11, bf16[768,768]{1,0:T(8,128)(2,1)} %bitcast.12, ...), custom_call_target="tpu_custom_call" | custom-call | tf_op jit(solution)/shard_map/dit_steps/pallas_call | solution.py:451
  50.0 1.4 %copy.15 = f32[2,128,48]{1,2,0:T(8,128)} copy(f32[2,128,48]{1,2,0:T(8,128)} %bitcast.17) | data formatting | bytes 98304
  51.4 1.8 %copy.16 = bf16[1,2,128,768]{3,2,1,0:T(8,128)(2,1)} copy(bf16[1,2,128,768]{3,2,1,0:T(8,128)(2,1)} %bitcast.13) | data formatting | bytes 786432

commit v2 on v1

--- a/solution.py
+++ b/solution.py
@@ -51,10 +51,10 @@
 
 
 def kernel(x_hbm, h_hbm, win_hbm, wout_hbm, wqkv_hbm, wo_hbm, wup_hbm, wdown_hbm, mod_hbm, alpha_ref, beta_ref,
-           xo_ref, ho_hbm,
-           wqkv, wo, wup, wdown, win, wout, mod, xraw, hin, outb, xbt, xbt_out, xs, xfin_out, xfin,
+           xo_ref, ho_ref,
+           wqkv, wo, wup, wdown, win, wout, mod, xraw, xsend, hsend, hin, outb, xbt, xbt_out, xs, xfin_out, xfin,
            hres, unorm, qs, ks, vt, attn, act, s_a, s_b, p_a, p_b,
-           w_sem, small_sem, init_send, init_recv, st_send, st_recv, x_send, x_recv, xf_send, xf_recv, ho_sem, ho_send, ho_recv, go_sem):
+           w_sem, small_sem, init_send, init_recv, st_send, st_recv, x_send, x_recv, xf_send, xf_recv, ho_send, ho_recv, go_sem):
     y = lax.axis_index("seq")
     s = lax.axis_index("stage")
     z = lax.axis_index("data")
@@ -81,13 +81,17 @@
     cp_rest = [local(wo_hbm, wo, w_sem.at[3])]
     cp_rest += [local(wup_hbm.at[:, pl.ds(j * DIM, DIM)], wup.at[j], w_sem.at[4 + j]) for j in range(4)]
     cp_rest += [local(wdown_hbm, wdown, w_sem.at[8])]
-    rc_h = remote(h_hbm.at[h_idx, oy], hin.at[0, 0], init_send.at[0], init_recv.at[0], oy, s)
-    rc_x = remote(x_hbm.at[oy], xraw.at[0], init_send.at[1], init_recv.at[1], oy, s)
+    cp_hs = local(h_hbm.at[h_idx, oy], hsend, small_sem.at[5])
+    cp_xs = local(x_hbm.at[oy], xsend, small_sem.at[6])
+    rc_h = remote(hsend, hin.at[0, 0], init_send.at[0], init_recv.at[0], oy, s)
+    rc_x = remote(xsend, xraw.at[0], init_send.at[1], init_recv.at[1], oy, s)
 
     @pl.when(jnp.logical_not(is_first))
     def _():
+        cp_hs.start()
         cp_h.start()
 
+    cp_xs.start()
     cp_x.start()
     cp_mod.start()
     cp_win.start()
@@ -101,6 +105,12 @@
             if dy == 0 and ds == 0:
                 continue
             pl.semaphore_signal(barrier, inc=1, device_id=(z, (y + dy) % 2, (s + ds) % STAGES), device_id_type=MESH)
+    cp_xs.wait()
+
+    @pl.when(jnp.logical_not(is_first))
+    def _():
+        cp_hs.wait()
+
     pl.semaphore_wait(barrier, 2 * STAGES - 1)
 
     @pl.when(uses_x)
@@ -274,11 +284,11 @@
         if c == 0:
             @pl.when(k == STEPS - 1)
             def _():
-                remote(outb.at[k, c], ho_hbm.at[y], ho_send, ho_recv, oy, s).start()
+                remote(outb.at[k, c], ho_ref.at[y], ho_send, ho_recv, oy, s).start()
         else:
             @pl.when(k == STEPS - 1)
             def _():
-                local(outb.at[k, c], ho_hbm.at[y], ho_sem).start()
+                ho_ref[y] = outb[k, c]
 
         @pl.when(is_last)
         def _():
@@ -395,10 +405,17 @@
     def _():
         rc_x.wait_send()
 
-    local(outb.at[STEPS - 1, 1], ho_hbm.at[y], ho_sem).wait()
-    last = remote(outb.at[STEPS - 1, 0], ho_hbm.at[oy], ho_send, ho_recv, oy, s)
+    last = remote(outb.at[STEPS - 1, 0], ho_ref.at[oy], ho_send, ho_recv, oy, s)
     last.wait_send()
     last.wait_recv()
+
+
+def writer(x_ref, h_ref, xo_ref, ho_ref, sems):
+    copies = [pltpu.make_async_copy(x_ref, xo_ref, sems.at[0]), pltpu.make_async_copy(h_ref, ho_ref, sems.at[1])]
+    for copy in copies:
+        copy.start()
+    for copy in copies:
+        copy.wait()
 
 
 def solution(mesh):
@@ -415,6 +432,8 @@
         pltpu.VMEM((LAT, DIM), BF16),
         pltpu.VMEM((STEPS, 6, 1, DIM), F32),
         pltpu.VMEM((2, LAT, ROWS), F32),
+        pltpu.VMEM((LAT, ROWS), F32),
+        pltpu.VMEM((ROWS, DIM), BF16),
         pltpu.VMEM((STEPS, 2, ROWS, DIM), BF16),
         pltpu.VMEM((STEPS, 2, ROWS, DIM), BF16),
         pltpu.VMEM((STEPS, 2, LAT, ROWS), BF16),
@@ -433,23 +452,31 @@
         pltpu.VMEM((2 * ROWS, 2 * ROWS), F32),
         pltpu.VMEM((2 * ROWS, 2 * ROWS), BF16),
         pltpu.VMEM((2 * ROWS, 2 * ROWS), BF16),
-        dma((9,)), dma((5,)), dma((2,)), dma((2,)),
+        dma((9,)), dma((7,)), dma((2,)), dma((2,)),
         dma((STEPS - 1, 2)), dma((STEPS - 1, 2)), dma((STEPS - 1, 2)), dma((STEPS - 1, 2)),
-        dma((2 * STAGES - 1,)), dma((2,)), dma, dma, dma, pltpu.SemaphoreType.REGULAR,
+        dma((2 * STAGES - 1,)), dma((2,)), dma, dma, pltpu.SemaphoreType.REGULAR,
     ]
 
     def device_fn(x_init, h_init, w_in, w_out, w_qkv, w_o, w_up, w_down, ada_mod, alpha_coef, beta_coef):
         call = pl.pallas_call(
             kernel,
             name="dit_steps",
-            out_shape=(jax.ShapeDtypeStruct((2, LAT, ROWS), F32), jax.ShapeDtypeStruct((2, ROWS, DIM), BF16)),
+            out_shape=(pltpu.VMEM((2, LAT, ROWS), F32), pltpu.VMEM((2, ROWS, DIM), BF16)),
             in_specs=[hbm] * 9 + [smem] * 2,
-            out_specs=(vmem, hbm),
+            out_specs=(vmem, vmem),
             scratch_shapes=scratch,
-            compiler_params=pltpu.CompilerParams(collective_id=0, has_side_effects=True, vmem_limit_bytes=60 * 1024 * 1024),
+            compiler_params=pltpu.CompilerParams(collective_id=0, has_side_effects=True, vmem_limit_bytes=58 * 1024 * 1024),
         )
         x_final, h_final = call(x_init.swapaxes(1, 2), h_init, w_in, w_out.T, w_qkv.reshape(DIM, 3 * DIM), w_o.reshape(DIM, DIM),
                                 w_up.reshape(DIM, FF), w_down.reshape(FF, DIM), ada_mod.swapaxes(1, 2), alpha_coef, beta_coef)
+        x_final, h_final = pl.pallas_call(
+            writer,
+            name="write_out",
+            out_shape=(jax.ShapeDtypeStruct(x_final.shape, F32), jax.ShapeDtypeStruct(h_final.shape, BF16)),
+            in_specs=[vmem] * 2,
+            out_specs=(hbm, hbm),
+            scratch_shapes=[dma((2,))],
+        )(pltpu.with_memory_space_constraint(x_final, pltpu.VMEM), pltpu.with_memory_space_constraint(h_final, pltpu.VMEM))
         return x_final.swapaxes(1, 2), h_final[None]
 
     weight_spec = P("stage", None, None)

time: 53.4 us -> 50.2 us (0.940)
  local copies, waits for them, and re-layouts: 3.19 us -> 0 us
    unnamed x2 -> x0, local copies, waits for them, and re-layouts: 3.19 us -> none
    pallas_call x0 -> x1, Pallas kernels: none -> 0.78 us  [device_fn(): pl.pallas_call(writer, name='write_out', out_shape=(jax.ShapeDtypeStruct(...]
    pallas_call x1, Pallas kernels: 49.4 us -> 48.7 us  [device_fn(): call(x_init.swapaxes(1, 2), h_init, w_in, w_out.T, w_qkv.reshape(DIM, 3 *...]
where the time goes in v2:
time: 50.2 us; the launch traced here: 50.1 us
  Pallas kernels  49.5 us (99%)
  between operations  0.64 us (1%)
    pallas_call x1, Pallas kernels, device_fn(): call(x_init.swapaxes(1, 2), h_init, w_in, w_out.T, w_qkv.reshape(DIM, 3 *...  48.7 us

profile of v2, /device:TPU:0, one launch (start us, length us, event | category | flops | bytes accessed | tf_op | source)
XLA Modules:
  0.0 50.1 jit_solution(13171509475600244769)
XLA Ops:
  0.6 48.7 %dit_steps.1 = (f32[2,48,128]{2,1,0:T(8,128)S(1)}, bf16[2,128,768]{2,1,0:T(8,128)(2,1)S(1)}) custom-call(f32[2,48,128]{2,1,0:T(8,128)} %bitcast.15, bf16[3,2,128,768]{3,2,1,0:T(8,128)(2,1)} %h_hbm.1, bf16[48,768]{1,0:T(8,128)(2,1)} %win_hbm.1, bf16[48,768]{1,0:T(8,128)(2,1)} %bitcast.13, bf16[768,2304]{1,0:T(8,128)(2,1)} %bitcast.11, ...), custom_call_target="tpu_custom_call" | custom-call | tf_op jit(solution)/shard_map/dit_steps/pallas_call | solution.py:470
  49.4 0.8 %write_out.1 = (f32[2,48,128]{2,1,0:T(8,128)}, bf16[2,128,768]{2,1,0:T(8,128)(2,1)}) custom-call(f32[2,48,128]{2,1,0:T(8,128)S(1)} %get-tuple-element.6.x_ref, bf16[2,128,768]{2,1,0:T(8,128)(2,1)S(1)} %get-tuple-element.7.h_ref), custom_call_target="tpu_custom_call" | custom-call | tf_op jit(solution)/shard_map/write_out/pallas_call | solution.py:472

commit v3 on v2

--- a/solution.py
+++ b/solution.py
@@ -53,7 +53,7 @@
 def kernel(x_hbm, h_hbm, win_hbm, wout_hbm, wqkv_hbm, wo_hbm, wup_hbm, wdown_hbm, mod_hbm, alpha_ref, beta_ref,
            xo_ref, ho_ref,
            wqkv, wo, wup, wdown, win, wout, mod, xraw, xsend, hsend, hin, outb, xbt, xbt_out, xs, xfin_out, xfin,
-           hres, unorm, qs, ks, vt, attn, act, s_a, s_b, p_a, p_b,
+           hres, unorm, qs, ks, vt, attn, act, s_scr, p_scr,
            w_sem, small_sem, init_send, init_recv, st_send, st_recv, x_send, x_recv, xf_send, xf_recv, ho_send, ho_recv, go_sem):
     y = lax.axis_index("seq")
     s = lax.axis_index("stage")
@@ -198,8 +198,8 @@
             return run
         return [piece(n) for n in range(0, DIM, 256)]
 
-    def attn_pieces(c):
-        s_scr, p_scr = (s_a, s_b), (p_a, p_b)
+    def attn_units(c):
+        mxs, invs = {}, {}
 
         def scores(p):
             cols = slice(p * 128, (p + 1) * 128)
@@ -207,31 +207,32 @@
             zero = jnp.zeros_like(q2)
             qq = jnp.concatenate([jnp.where(lane < HD, q2, zero), jnp.where(lane < HD, zero, q2)], axis=0)
             k2 = jnp.concatenate([ks[0, :, cols], ks[1, :, cols]], axis=0)
-            s_scr[p % 2][...] = lax.dot_general(k2, qq, (((1,), (1,)), ((), ())), preferred_element_type=F32)
-
-        def softmax(p, half):
+            st = lax.dot_general(k2, qq, (((1,), (1,)), ((), ())), preferred_element_type=F32)
+            s_scr[c, p] = st
+            mxs[p] = jnp.max(st, axis=0, keepdims=True)
+
+        def exps(p, half):
             cols = slice(half * ROWS, (half + 1) * ROWS)
-            st = s_scr[p % 2][:, cols]
-            mx = jnp.max(st, axis=0, keepdims=True)
-            ex = jnp.exp2((st - mx) * EXP2_SCALE)
+            ex = jnp.exp2((s_scr[c, p, :, cols] - mxs[p][:, cols]) * EXP2_SCALE)
             inv = 1.0 / jnp.sum(ex, axis=0, keepdims=True)
-            p_scr[p % 2][:, cols] = (ex * inv).astype(BF16)
+            p_scr[c, p, :, cols] = (ex * inv).astype(BF16)
 
         def values(p):
             cols = slice(p * 128, (p + 1) * 128)
             v2 = jnp.concatenate([vt[0, cols, :], vt[1, cols, :]], axis=1)
-            ot = mm(v2, p_scr[p % 2][...])
+            ot = mm(v2, p_scr[c, p])
             o2 = jnp.concatenate([ot[:HD, :ROWS], ot[HD:, ROWS:]], axis=0)
             attn[c, :, cols] = o2.T.astype(BF16)
 
-        pieces = [functools.partial(scores, 0)]
+        sc = [functools.partial(scores, p) for p in range(PAIRS)]
+        ev = []
         for p in range(PAIRS):
-            if p + 1 < PAIRS:
-                pieces.append(functools.partial(scores, p + 1))
-            pieces.append(functools.partial(softmax, p, 0))
-            pieces.append(functools.partial(softmax, p, 1))
-            pieces.append(functools.partial(values, p))
-        return pieces
+            ev.append(functools.partial(exps, p, 0))
+            ev.append(functools.partial(exps, p, 1))
+            if p:
+                ev.append(functools.partial(values, p - 1))
+        ev.append(functools.partial(values, PAIRS - 1))
+        return sc, ev
 
     def wo_pieces(c):
         def piece(n):
@@ -356,15 +357,17 @@
         interleave(q_pieces(ca), ln1_pieces(k, cb))
         interleave(k_pieces(cb))
         interleave(q_pieces(cb))
-        interleave(v_pieces(cb))
-        interleave(attn_pieces(0))
-        att1 = attn_pieces(1)
-        interleave(wo_pieces(0) + ln2_pieces(k, 0), att1[:8])
-        interleave(up_pieces(0))
-        interleave(down_pieces(k, 0), att1[8:])
+        sc0, ev0 = attn_units(0)
+        sc1, ev1 = attn_units(1)
+        interleave(sc0[:2])
+        interleave(v_pieces(cb) + sc0[2:] + sc1, ev0)
+        interleave(wo_pieces(0), ev1[:3])
+        interleave(ln2_pieces(k, 0), ev1[3:5])
+        interleave(up_pieces(0), ev1[5:10])
+        down0 = down_pieces(k, 0)
+        interleave(down0[:2], ev1[10:] + wo_pieces(1))
+        interleave(down0[2:], ln2_pieces(k, 1))
         finish(k, 0)
-        interleave(wo_pieces(1))
-        interleave(ln2_pieces(k, 1))
         interleave(up_pieces(1))
         interleave(down_pieces(k, 1))
         finish(k, 1)
@@ -448,10 +451,8 @@
         pltpu.VMEM((2, DIM, ROWS), BF16),
         pltpu.VMEM((2, ROWS, DIM), BF16),
         pltpu.VMEM((2, ROWS, FF), BF16),
-        pltpu.VMEM((2 * ROWS, 2 * ROWS), F32),
-        pltpu.VMEM((2 * ROWS, 2 * ROWS), F32),
-        pltpu.VMEM((2 * ROWS, 2 * ROWS), BF16),
-        pltpu.VMEM((2 * ROWS, 2 * ROWS), BF16),
+        pltpu.VMEM((2, HEADS // 2, 2 * ROWS, 2 * ROWS), F32),
+        pltpu.VMEM((2, HEADS // 2, 2 * ROWS, 2 * ROWS), BF16),
         dma((9,)), dma((7,)), dma((2,)), dma((2,)),
         dma((STEPS - 1, 2)), dma((STEPS - 1, 2)), dma((STEPS - 1, 2)), dma((STEPS - 1, 2)),
         dma((2 * STAGES - 1,)), dma((2,)), dma, dma, pltpu.SemaphoreType.REGULAR,

time: 50.2 us -> 48.1 us (0.958)
  Pallas kernels: 49.5 us -> 47.3 us
    pallas_call x1, Pallas kernels: 48.7 us -> 46.6 us  [device_fn(): call(x_init.swapaxes(1, 2), h_init, w_in, w_out.T, w_qkv.reshape(DIM, 3 *...]
where the time goes in v3:
time: 48.1 us; the launch traced here: 48 us
  Pallas kernels  47.3 us (98%)
  between operations  0.64 us (1%)
    pallas_call x1, Pallas kernels, device_fn(): call(x_init.swapaxes(1, 2), h_init, w_in, w_out.T, w_qkv.reshape(DIM, 3 *...  46.6 us

profile of v3, /device:TPU:0, one launch (start us, length us, event | category | flops | bytes accessed | tf_op | source)
XLA Modules:
  0.0 48.0 jit_solution(14143041629580307576)
XLA Ops:
  0.6 46.6 %dit_steps.1 = (f32[2,48,128]{2,1,0:T(8,128)S(1)}, bf16[2,128,768]{2,1,0:T(8,128)(2,1)S(1)}) custom-call(f32[2,48,128]{2,1,0:T(8,128)} %bitcast.15, bf16[3,2,128,768]{3,2,1,0:T(8,128)(2,1)} %h_hbm.1, bf16[48,768]{1,0:T(8,128)(2,1)} %win_hbm.1, bf16[48,768]{1,0:T(8,128)(2,1)} %bitcast.13, bf16[768,2304]{1,0:T(8,128)(2,1)} %bitcast.11, ...), custom_call_target="tpu_custom_call" | custom-call | tf_op jit(solution)/shard_map/dit_steps/pallas_call | solution.py:471
  47.2 0.8 %write_out.1 = (f32[2,48,128]{2,1,0:T(8,128)}, bf16[2,128,768]{2,1,0:T(8,128)(2,1)}) custom-call(f32[2,48,128]{2,1,0:T(8,128)S(1)} %get-tuple-element.6.x_ref, bf16[2,128,768]{2,1,0:T(8,128)(2,1)S(1)} %get-tuple-element.7.h_ref), custom_call_target="tpu_custom_call" | custom-call | tf_op jit(solution)/shard_map/write_out/pallas_call | solution.py:473

commit v4 on v3

--- a/solution.py
+++ b/solution.py
@@ -209,11 +209,14 @@
             k2 = jnp.concatenate([ks[0, :, cols], ks[1, :, cols]], axis=0)
             st = lax.dot_general(k2, qq, (((1,), (1,)), ((), ())), preferred_element_type=F32)
             s_scr[c, p] = st
-            mxs[p] = jnp.max(st, axis=0, keepdims=True)
+            if c == 0:
+                mxs[p] = jnp.max(st, axis=0, keepdims=True)
 
         def exps(p, half):
             cols = slice(half * ROWS, (half + 1) * ROWS)
-            ex = jnp.exp2((s_scr[c, p, :, cols] - mxs[p][:, cols]) * EXP2_SCALE)
+            st = s_scr[c, p, :, cols]
+            mx = mxs[p][:, cols] if p in mxs else jnp.max(st, axis=0, keepdims=True)
+            ex = jnp.exp2((st - mx) * EXP2_SCALE)
             inv = 1.0 / jnp.sum(ex, axis=0, keepdims=True)
             p_scr[c, p, :, cols] = (ex * inv).astype(BF16)
 
@@ -225,14 +228,9 @@
             attn[c, :, cols] = o2.T.astype(BF16)
 
         sc = [functools.partial(scores, p) for p in range(PAIRS)]
-        ev = []
-        for p in range(PAIRS):
-            ev.append(functools.partial(exps, p, 0))
-            ev.append(functools.partial(exps, p, 1))
-            if p:
-                ev.append(functools.partial(values, p - 1))
-        ev.append(functools.partial(values, PAIRS - 1))
-        return sc, ev
+        ex = [functools.partial(exps, p, half) for p in range(PAIRS) for half in range(2)]
+        va = [functools.partial(values, p) for p in range(PAIRS)]
+        return sc, ex, va
 
     def wo_pieces(c):
         def piece(n):
@@ -326,6 +324,11 @@
         def _():
             x_copy(kprev, ca).wait_recv()
 
+        spare = k // 64
+
+        def hold_scores(n):
+            s_scr[1, PAIRS + spare, 0:16, 0:128] = act[0, 0:16, n * 256:n * 256 + 128].astype(F32)
+
         embed(k, ca)
         interleave(ln1_pieces(k, ca))
         interleave(k_pieces(ca) + v_pieces(ca))
@@ -357,15 +360,23 @@
         interleave(q_pieces(ca), ln1_pieces(k, cb))
         interleave(k_pieces(cb))
         interleave(q_pieces(cb))
-        sc0, ev0 = attn_units(0)
-        sc1, ev1 = attn_units(1)
-        interleave(sc0[:2])
-        interleave(v_pieces(cb) + sc0[2:] + sc1, ev0)
-        interleave(wo_pieces(0), ev1[:3])
-        interleave(ln2_pieces(k, 0), ev1[3:5])
-        interleave(up_pieces(0), ev1[5:10])
+        sc0, ex0, va0 = attn_units(0)
+        sc1, ex1, va1 = attn_units(1)
+        vb = v_pieces(cb)
+        interleave(sc0[:2] + [vb[0]] + sc0[2:4] + [vb[1]] + sc0[4:] + [vb[2]], ex0[:6])
+        interleave([piece for pair in zip(sc1, va0) for piece in pair], ex0[6:])
+        interleave(wo_pieces(0))
+        interleave(ln2_pieces(k, 0))
+        up0 = up_pieces(0)
         down0 = down_pieces(k, 0)
-        interleave(down0[:2], ev1[10:] + wo_pieces(1))
+        for p in range(3):
+            interleave(up0[3 * p:3 * p + 3])
+            hold_scores(3 * p + 2)
+            interleave(ex1[2 * p:2 * p + 2])
+        interleave(up0[9:])
+        hold_scores(11)
+        interleave(down0[:2], ex1[6:])
+        interleave(va1 + wo_pieces(1))
         interleave(down0[2:], ln2_pieces(k, 1))
         finish(k, 0)
         interleave(up_pieces(1))
@@ -451,7 +462,7 @@
         pltpu.VMEM((2, DIM, ROWS), BF16),
         pltpu.VMEM((2, ROWS, DIM), BF16),
         pltpu.VMEM((2, ROWS, FF), BF16),
-        pltpu.VMEM((2, HEADS // 2, 2 * ROWS, 2 * ROWS), F32),
+        pltpu.VMEM((2, HEADS // 2 + 1, 2 * ROWS, 2 * ROWS), F32),
         pltpu.VMEM((2, HEADS // 2, 2 * ROWS, 2 * ROWS), BF16),
         dma((9,)), dma((7,)), dma((2,)), dma((2,)),
         dma((STEPS - 1, 2)), dma((STEPS - 1, 2)), dma((STEPS - 1, 2)), dma((STEPS - 1, 2)),

time: 48.1 us -> 49.1 us (1.021)
  Pallas kernels: 47.3 us -> 48.4 us
    pallas_call x1, Pallas kernels: 46.6 us -> 47.6 us  [device_fn(): call(x_init.swapaxes(1, 2), h_init, w_in, w_out.T, w_qkv.reshape(DIM, 3 *...]
where the time goes in v4:
time: 49.1 us; the launch traced here: 49 us
  Pallas kernels  48.4 us (99%)
  between operations  0.64 us (1%)
    pallas_call x1, Pallas kernels, device_fn(): call(x_init.swapaxes(1, 2), h_init, w_in, w_out.T, w_qkv.reshape(DIM, 3 *...  47.6 us

profile of v4, /device:TPU:0, one launch (start us, length us, event | category | flops | bytes accessed | tf_op | source)
XLA Modules:
  0.0 49.0 jit_solution(9780217642530518836)
XLA Ops:
  0.6 47.6 %dit_steps.1 = (f32[2,48,128]{2,1,0:T(8,128)S(1)}, bf16[2,128,768]{2,1,0:T(8,128)(2,1)S(1)}) custom-call(f32[2,48,128]{2,1,0:T(8,128)} %bitcast.15, bf16[3,2,128,768]{3,2,1,0:T(8,128)(2,1)} %h_hbm.1, bf16[48,768]{1,0:T(8,128)(2,1)} %win_hbm.1, bf16[48,768]{1,0:T(8,128)(2,1)} %bitcast.13, bf16[768,2304]{1,0:T(8,128)(2,1)} %bitcast.11, ...), custom_call_target="tpu_custom_call" | custom-call | tf_op jit(solution)/shard_map/dit_steps/pallas_call | solution.py:482
  48.2 0.8 %write_out.1 = (f32[2,48,128]{2,1,0:T(8,128)}, bf16[2,128,768]{2,1,0:T(8,128)(2,1)}) custom-call(f32[2,48,128]{2,1,0:T(8,128)S(1)} %get-tuple-element.6.x_ref, bf16[2,128,768]{2,1,0:T(8,128)(2,1)S(1)} %get-tuple-element.7.h_ref), custom_call_target="tpu_custom_call" | custom-call | tf_op jit(solution)/shard_map/write_out/pallas_call | solution.py:484
